TPU v7x, 32 devices: a whole 2x2x4 slice. The times are simulated.
32 devices in a mesh: groups: 2 (over y), seq: 4 (over z), batch: 2 (over x), head: 2 (over core).
Axes of the slice: x: 2, y: 2, z: 4, core: 2. Of those that a mesh axis runs over, the one named last changes fastest.
Arguments:
- queries: bfloat16 [64, 64, 128], P(('groups', 'seq', 'batch'), 'head'), parts along dimension 0, may hold values from -16 to 16
- fresh_token_keys: bfloat16 [64, 8, 128], P(('groups', 'seq', 'batch'), 'head'), parts along dimension 0, may hold values from -12 to 12
- fresh_token_values: bfloat16 [64, 8, 128], P(('groups', 'seq', 'batch'), 'head'), parts along dimension 0, may hold values from -6 to 6
- shared_prefix_keys: bfloat16 [16384, 8, 128], P(('groups', 'seq'), 'head'), parts along dimension 0, may hold values from -6 to 6
- shared_prefix_values: bfloat16 [16384, 8, 128], P(('groups', 'seq'), 'head'), parts along dimension 0, may hold values from -6 to 6
- sequence_suffix_keys: bfloat16 [64, 192, 8, 128], P(('groups', 'seq', 'batch'), None, 'head'), parts along dimension 0, may hold values from -8 to 8
- sequence_suffix_values: bfloat16 [64, 192, 8, 128], P(('groups', 'seq', 'batch'), None, 'head'), parts along dimension 0, may hold values from -6 to 6
- suffix_lengths: int32 [64], P(('groups', 'seq', 'batch')), parts along dimension 0, may hold values from 0 to 192, as said below
Outputs:
- context: bfloat16 [64, 64, 128], P(('groups', 'seq', 'batch'), 'head'), parts along dimension 0
There are 2 independent parts, one for each index of `groups`. A program takes and returns all parts, laid end to end along the dimension named above; each array names one. Nothing has to cross between parts.
Inputs may be any that keep to these rules, and one draw needn't show every extreme that they name: `suffix_lengths`: slots at and beyond a sequence's length hold no token. Some sequence has all 192 slots live in every draw.
All inputs are finite; a program needn't handle non-finite values.
Results may differ from a plain program's by a relative error of at most 0.002.
Values may be sent and summed in bfloat16 or wider, within the bound.
A program may use at most 64 MiB of HBM per device.

v0:
```python
import math
import jax
import jax.numpy as jnp
from jax import lax
from jax.sharding import PartitionSpec as P


def prefix_block(query_rows, block_keys, block_values, inv_root):
    scores = (
        lax.dot_general(
            query_rows, block_keys, (((1,), (1,)), ((), ())), preferred_element_type=jnp.float32
        )
        * inv_root
    )
    maxima = jnp.max(scores, axis=1)
    weights = jnp.exp(scores - maxima[:, None]).astype(jnp.bfloat16)
    totals = jnp.sum(weights, axis=1, dtype=jnp.float32)
    outputs = jnp.dot(weights, block_values, preferred_element_type=jnp.float32)
    return (maxima, totals, outputs)


def body(
    queries,
    fresh_token_keys,
    fresh_token_values,
    shared_prefix_keys,
    shared_prefix_values,
    sequence_suffix_keys,
    sequence_suffix_values,
    suffix_lengths,
):
    own_count, head_count, width = queries.shape
    kv_count = shared_prefix_keys.shape[1]
    query_group = head_count // kv_count
    inv_root = 1.0 / math.sqrt(width)
    seq_count = lax.axis_size("seq")
    gathered = lax.all_gather(queries, "seq", axis=0, tiled=True)
    row_count = gathered.shape[0]
    grouped = gathered.reshape(row_count, kv_count, query_group, width)
    maxima_list = []
    totals_list = []
    outputs_list = []
    for kv_head in range(kv_count):
        query_rows = grouped[:, kv_head].reshape(row_count * query_group, width)
        maxima, totals, outputs = prefix_block(
            query_rows, shared_prefix_keys[:, kv_head], shared_prefix_values[:, kv_head], inv_root
        )
        maxima_list.append(maxima.reshape(row_count, query_group))
        totals_list.append(totals.reshape(row_count, query_group))
        outputs_list.append(outputs.reshape(row_count, query_group, width))
    block_max = jnp.stack(maxima_list, axis=1).reshape(row_count, head_count)
    block_total = jnp.stack(totals_list, axis=1).reshape(row_count, head_count)
    block_out = jnp.stack(outputs_list, axis=1).reshape(row_count, head_count, width)
    own_rows = queries.reshape(own_count, kv_count, query_group, width)
    own_scores = (
        jnp.einsum("bgqd,bgd->bgq", own_rows, fresh_token_keys, preferred_element_type=jnp.float32)
        * inv_root
    )
    recent = (
        jnp.einsum(
            "bgqd,bsgd->bgqs", own_rows, sequence_suffix_keys, preferred_element_type=jnp.float32
        )
        * inv_root
    )
    slot_count = sequence_suffix_keys.shape[1]
    live = (jnp.arange(slot_count, dtype=jnp.int32)[None, :] < suffix_lengths[:, None])[
        :, None, None, :
    ]
    local_max = jnp.maximum(
        own_scores, jnp.max(jnp.where(live, recent, own_scores[..., None]), axis=-1)
    )
    recent_weights = jnp.where(
        live, jnp.exp(jnp.where(live, recent - local_max[..., None], 0.0)), 0.0
    ).astype(jnp.bfloat16)
    own_weights = jnp.exp(own_scores - local_max).astype(jnp.bfloat16)
    local_total = jnp.sum(recent_weights, axis=-1, dtype=jnp.float32) + own_weights.astype(
        jnp.float32
    )
    local_out = jnp.einsum(
        "bgqs,bsgd->bgqd",
        recent_weights,
        sequence_suffix_values,
        preferred_element_type=jnp.float32,
    )
    local_out = (
        local_out
        + own_weights.astype(jnp.float32)[..., None]
        * fresh_token_values.astype(jnp.float32)[:, :, None, :]
    )
    local_max = local_max.reshape(own_count, head_count)
    local_total = local_total.reshape(own_count, head_count)
    local_out = local_out.reshape(own_count, head_count, width)
    state_shape = (seq_count, own_count, head_count)
    got_out, got_max, got_total = (
        lax.all_to_all(
            block_out.reshape(seq_count, own_count, head_count, width),
            "seq",
            split_axis=0,
            concat_axis=0,
            tiled=True,
        ),
        lax.all_to_all(
            block_max.reshape(state_shape), "seq", split_axis=0, concat_axis=0, tiled=True
        ),
        lax.all_to_all(
            block_total.reshape(state_shape), "seq", split_axis=0, concat_axis=0, tiled=True
        ),
    )
    highest = jnp.maximum(local_max, jnp.max(got_max, axis=0))
    block_scale = jnp.exp(got_max - highest[None])
    local_scale = jnp.exp(local_max - highest)
    total = local_total * local_scale + jnp.sum(got_total * block_scale, axis=0)
    numerator = local_out * local_scale[..., None] + jnp.sum(
        got_out * block_scale[..., None], axis=0
    )
    return (numerator / total[..., None]).astype(jnp.bfloat16)


def solution(mesh):
    in_specs = (
        P(("groups", "seq", "batch"), "head", None),
        P(("groups", "seq", "batch"), "head", None),
        P(("groups", "seq", "batch"), "head", None),
        P(("groups", "seq"), "head", None),
        P(("groups", "seq"), "head", None),
        P(("groups", "seq", "batch"), None, "head", None),
        P(("groups", "seq", "batch"), None, "head", None),
        P(("groups", "seq", "batch")),
    )
    out_specs = P(("groups", "seq", "batch"), "head", None)
    return jax.shard_map(body, mesh=mesh, in_specs=in_specs, out_specs=out_specs, check_vma=False)
```

profile of v0, /device:TPU:0, one launch (start us, length us, event | category | flops | bytes accessed | tf_op | source)
XLA Modules:
  0.0 72.7 jit_solution(282723957632736956)
XLA Ops:
  0.0 8.9 %fusion.19 = (bf16[2048,1,128]{2,1,0:T(2,128)(2,1)S(1)}, bf16[2048,1,128]{2,1,0:T(2,128)(2,1)}, bf16[2048,1,128]{2,1,0:T(2,128)(2,1)}, bf16[2048,1,128]{2,1,0:T(2,128)(2,1)}) fusion(bf16[2048,4,128]{2,1,0:T(4,128)(2,1)} %param.11), kind=kLoop, calls=%fused_computation.62 | loop fusion | bytes 4194304 | tf_op jit(solution)/shard_map/slice | solution.py:46
  8.9 15.1 %all_gather.3 = bf16[16,32,128]{2,1,0:T(8,128)(2,1)S(1)} all-gather(bf16[4,32,128]{2,1,0:T(8,128)(2,1)S(1)} %copy-done.5), channel_id=1, replica_groups=mesh['groups'=2,'seq'=4,'batch'=2,'head'=2] {'seq'}, dimensions={0}, use_global_device_ids=true | all-gather | bytes 163840 | tf_op jit(solution)/shard_map/all_gather | solution.py:37
  24.0 0.4 fusion.24
  24.8 1.6 %fusion.23 = (f32[128]{0:T(128)S(1)}, f32[128,2048]{1,0:T(8,128)S(1)}) fusion(bf16[2048,1,128]{2,1,0:T(2,128)(2,1)} %get-tuple-element.13, bf16[16,4,8,128]{3,2,1,0:T(8,128)(2,1)S(1)} %bitcast.99), kind=kOutput, calls=%fused_computation.66 | convolution fusion | flops 67633024 | bytes 1606144 | tf_op jit(solution)/shard_map/dot_general | solution.py:10
  26.8 1.6 %fusion.22 = (f32[128]{0:T(128)S(1)}, f32[128,2048]{1,0:T(8,128)S(1)}) fusion(bf16[2048,1,128]{2,1,0:T(2,128)(2,1)} %get-tuple-element.12, bf16[16,4,8,128]{3,2,1,0:T(8,128)(2,1)S(1)} %bitcast.100), kind=kOutput, calls=%fused_computation.65 | convolution fusion | flops 67633024 | bytes 1606144 | tf_op jit(solution)/shard_map/dot_general | solution.py:10
  28.4 1.0 %copy-done.1 = f32[128,2048]{1,0:T(8,128)} copy-done((f32[128,2048]{1,0:T(8,128)}, f32[128,2048]{1,0:T(8,128)S(1)}, u32[]{:S(2)}) %copy-start.1) | copy-done | bytes 1048600
  29.8 1.6 %fusion.21 = (f32[128]{0:T(128)S(1)}, f32[128,2048]{1,0:T(8,128)S(1)}) fusion(bf16[2048,1,128]{2,1,0:T(2,128)(2,1)} %get-tuple-element.14, bf16[16,4,8,128]{3,2,1,0:T(8,128)(2,1)S(1)} %bitcast.101), kind=kOutput, calls=%fused_computation.64 | convolution fusion | flops 67633024 | bytes 1606144 | tf_op jit(solution)/shard_map/dot_general | solution.py:10
  31.5 1.0 %copy-done.3 = f32[128,2048]{1,0:T(8,128)} copy-done((f32[128,2048]{1,0:T(8,128)}, f32[128,2048]{1,0:T(8,128)S(1)}, u32[]{:S(2)}) %copy-start.3) | copy-done | bytes 1048600
  33.0 0.7 reshape.116
  33.6 5.0 %all-to-all-start.2 = ((f32[4,1,128]{2,1,0:T(1,128)}), f32[4,1,128]{2,1,0:T(1,128)S(1)}, u32[]{:S(2)}, u32[]{:S(2)}) async-start(f32[4,1,128]{2,1,0:T(1,128)} %reshape.116), calls=%async_computation.2 | async-start | bytes 4096 | tf_op jit(solution)/shard_map/all_to_all | solution.py:105
  39.2 0.6 select_reduce_fusion
  40.0 8.1 %fusion.20 = (bf16[2048,1,128]{2,1,0:T(2,128)(2,1)S(1)}, bf16[2048,1,128]{2,1,0:T(2,128)(2,1)S(1)}, bf16[2048,1,128]{2,1,0:T(2,128)(2,1)S(1)}, bf16[2048,1,128]{2,1,0:T(2,128)(2,1)S(1)}) fusion(bf16[2048,4,128]{2,1,0:T(4,128)(2,1)} %param.12), kind=kLoop, calls=%fused_computation.63 | loop fusion | bytes 4194304 | tf_op jit(solution)/shard_map/slice | solution.py:46
  48.5 0.4 convolution_bitcast_fusion.2
  48.9 0.5 copy-done.2
  50.2 0.7 reshape.114
  50.9 5.1 %all-to-all-start = ((f32[4,1,128]{2,1,0:T(1,128)}), f32[4,1,128]{2,1,0:T(1,128)S(1)}, u32[]{:S(2)}, u32[]{:S(2)}) async-start(f32[4,1,128]{2,1,0:T(1,128)} %reshape.114), calls=%async_computation | async-start | bytes 4096 | tf_op jit(solution)/shard_map/all_to_all | solution.py:102
  56.2 0.7 copy.39
  56.9 0.5 broadcast.26
  57.4 0.7 reduce
  58.2 3.2 %all-to-all-done = f32[4,1,128]{2,1,0:T(1,128)S(1)} async-done(((f32[4,1,128]{2,1,0:T(1,128)}), f32[4,1,128]{2,1,0:T(1,128)S(1)}, u32[]{:S(2)}, u32[]{:S(2)}) %all-to-all-start) | async-done | bytes 2080 | tf_op jit(solution)/shard_map/all_to_all | solution.py:102
  61.4 3.4 %all-to-all-start.1 = ((f32[4,4,32,128]{3,2,1,0:T(8,128)}), f32[4,4,32,128]{3,2,1,0:T(8,128)S(1)}, u32[]{:S(2)}, u32[]{:S(2)}) async-start(f32[4,4,32,128]{3,2,1,0:T(8,128)} %bitcast.30), calls=%async_computation.1 | async-start | bytes 524288 | tf_op jit(solution)/shard_map/all_to_all | solution.py:95
  64.8 0.7 reduce.1
  65.6 5.9 %all-to-all-done.1 = f32[4,4,32,128]{3,2,1,0:T(8,128)S(1)} async-done(((f32[4,4,32,128]{3,2,1,0:T(8,128)}), f32[4,4,32,128]{3,2,1,0:T(8,128)S(1)}, u32[]{:S(2)}, u32[]{:S(2)}) %all-to-all-start.1) | async-done | bytes 262176 | tf_op jit(solution)/shard_map/all_to_all | solution.py:95
  71.7 1.0 %fusion.4 = bf16[4,32,128]{2,1,0:T(8,128)(2,1)} fusion(f32[4,32,128]{2,1,0:T(8,128)S(1)} %multiply_reduce_fusion, bf16[4,192,4,128]{3,2,1,0:T(4,128)(2,1)S(1)} %copy-done.7, f32[4,32]{1,0:T(4,128)S(1)} %get-tuple-element.5, f32[4,32]{1,0:T(4,128)S(1)} %get-tuple-element.6, f32[4,4,128]{2,1,0:T(4,128)S(1)} %convert_element_type.46, ...), kind=kOutput, calls=%fused_computation.14 | convolution fusion | flops 6488064 | bytes 994048 | tf_op jit(solution)/shard_map/bgqs,bsgd->bgqd/dot_general | solution.py:79
  (56 shorter events, 4.2 us)
Async XLA Ops:
  0.0 39.2 %copy-start = (bf16[4,192,4,128]{3,2,1,0:T(4,128)(2,1)S(1)}, bf16[4,192,4,128]{3,2,1,0:T(4,128)(2,1)}, u32[]{:S(2)}) copy-start(bf16[4,192,4,128]{3,2,1,0:T(4,128)(2,1)} %param.13) | copy-start | bytes 2359300
  0.0 8.9 %copy-start.5 = (bf16[4,32,128]{2,1,0:T(8,128)(2,1)S(1)}, bf16[4,32,128]{2,1,0:T(8,128)(2,1)}, u32[]{:S(2)}) copy-start(bf16[4,32,128]{2,1,0:T(8,128)(2,1)} %param.8) | copy-start | bytes 98308
  28.4 1.0 %copy-start.1 = (f32[128,2048]{1,0:T(8,128)}, f32[128,2048]{1,0:T(8,128)S(1)}, u32[]{:S(2)}) copy-start(f32[128,2048]{1,0:T(8,128)S(1)} %get-tuple-element.22) | copy-start | bytes 3145732
  28.4 10.5 %copy-start.8 = (bf16[4,4,128]{2,1,0:T(4,128)(2,1)S(1)}, bf16[4,4,128]{2,1,0:T(4,128)(2,1)}, u32[]{:S(2)}) copy-start(bf16[4,4,128]{2,1,0:T(4,128)(2,1)} %param.9) | copy-start | bytes 12292
  28.4 10.7 %copy-start.9 = (s32[4]{0:T(128)S(1)}, s32[4]{0:T(128)}, u32[]{:S(2)}) copy-start(s32[4]{0:T(128)} %param.15) | copy-start | bytes 52
  31.5 1.0 %copy-start.3 = (f32[128,2048]{1,0:T(8,128)}, f32[128,2048]{1,0:T(8,128)S(1)}, u32[]{:S(2)}) copy-start(f32[128,2048]{1,0:T(8,128)S(1)} %get-tuple-element.20) | copy-start | bytes 3145732
  33.6 17.3 %all-to-all-start.2 = ((f32[4,1,128]{2,1,0:T(1,128)}), f32[4,1,128]{2,1,0:T(1,128)S(1)}, u32[]{:S(2)}, u32[]{:S(2)}) async-start(f32[4,1,128]{2,1,0:T(1,128)} %reshape.116), calls=%async_computation.2 | async-start | bytes 4096 | tf_op jit(solution)/shard_map/all_to_all | solution.py:105
  48.1 1.2 %copy-start.2 = (f32[128,2048]{1,0:T(8,128)S(1)}, f32[128,2048]{1,0:T(8,128)}, u32[]{:S(2)}) copy-start(f32[128,2048]{1,0:T(8,128)} %copy-done.1) | copy-start | bytes 3145732
  48.1 1.6 %copy-start.4 = (f32[128,2048]{1,0:T(8,128)S(1)}, f32[128,2048]{1,0:T(8,128)}, u32[]{:S(2)}) copy-start(f32[128,2048]{1,0:T(8,128)} %copy-done.3) | copy-start | bytes 3145732
  49.4 7.5 %copy-start.6 = (bf16[4,4,128]{2,1,0:T(4,128)(2,1)S(1)}, bf16[4,4,128]{2,1,0:T(4,128)(2,1)}, u32[]{:S(2)}) copy-start(bf16[4,4,128]{2,1,0:T(4,128)(2,1)} %param.10) | copy-start | bytes 12292
  49.7 22.0 %copy-start.7 = (bf16[4,192,4,128]{3,2,1,0:T(4,128)(2,1)S(1)}, bf16[4,192,4,128]{3,2,1,0:T(4,128)(2,1)}, u32[]{:S(2)}) copy-start(bf16[4,192,4,128]{3,2,1,0:T(4,128)(2,1)} %param.14) | copy-start | bytes 2359300
  50.9 10.5 %all-to-all-start = ((f32[4,1,128]{2,1,0:T(1,128)}), f32[4,1,128]{2,1,0:T(1,128)S(1)}, u32[]{:S(2)}, u32[]{:S(2)}) async-start(f32[4,1,128]{2,1,0:T(1,128)} %reshape.114), calls=%async_computation | async-start | bytes 4096 | tf_op jit(solution)/shard_map/all_to_all | solution.py:102
  61.4 10.2 %all-to-all-start.1 = ((f32[4,4,32,128]{3,2,1,0:T(8,128)}), f32[4,4,32,128]{3,2,1,0:T(8,128)S(1)}, u32[]{:S(2)}, u32[]{:S(2)}) async-start(f32[4,4,32,128]{3,2,1,0:T(8,128)} %bitcast.30), calls=%async_computation.1 | async-start | bytes 524288 | tf_op jit(solution)/shard_map/all_to_all | solution.py:95
where the time goes:
time: 73.2 us; the launch traced here: 72.7 us
  local copies, waits for them, and re-layouts  23.3 us (32%)
  blocking collectives  15.1 us (21%)
  starting transfers between devices  13.5 us (18%)
  waiting for transfers between devices  9.17 us (13%)
  matrix products  8.4 us (11%)
  other arithmetic  3.07 us (4%)
    all_gather x1, blocking collectives, body(): gathered = lax.all_gather(queries, 'seq', axis=0, tiled=True)  15.1 us
    slice x1, local copies, waits for them, and re-layouts, body(): shared_prefix_keys[:, kv_head]  8.92 us
    slice x1, local copies, waits for them, and re-layouts, body(): shared_prefix_values[:, kv_head]  8.1 us
    all_to_all x1, waiting for transfers between devices, body(): lax.all_to_all(block_out.reshape(seq_count, own_count, head_count, width)...  5.93 us
    dot_general x4, matrix products, prefix_block(): lax.dot_general(query_rows, block_keys, (((1,), (1,)), ((), ())), preferr...  5.26 us
    all_to_all x1, starting transfers between devices, body(): lax.all_to_all(block_max.reshape(state_shape), 'seq', split_axis=0, conca...  5.09 us
    all_to_all x1, starting transfers between devices, body(): lax.all_to_all(block_total.reshape(state_shape), 'seq', split_axis=0, con...  4.97 us
    unnamed x24, local copies, waits for them, and re-layouts  4.02 us
  transfers between devices with their start and end apart: 3, of which 2 were waited for; matrix products, arithmetic and copies ran while one was open for 20% of the time, Pallas kernels for 0%

commit v1 on v0

--- a/solution.py
+++ b/solution.py
@@ -34,7 +34,8 @@
     query_group = head_count // kv_count
     inv_root = 1.0 / math.sqrt(width)
     seq_count = lax.axis_size("seq")
-    gathered = lax.all_gather(queries, "seq", axis=0, tiled=True)
+    outgoing = jnp.stack([queries] * lax.axis_size("seq"))
+    gathered = jnp.concatenate(lax.all_to_all(outgoing, "seq", 0, 0), axis=0)
     row_count = gathered.shape[0]
     grouped = gathered.reshape(row_count, kv_count, query_group, width)
     maxima_list = []

time: 73.2 us -> 68.7 us (0.939)
  blocking collectives: 15.1 us -> 0 us
  starting transfers between devices: 13.5 us -> 19.3 us
  matrix products: 8.4 us -> 14.1 us
  local copies, waits for them, and re-layouts: 23.3 us -> 18.9 us
  other arithmetic: 3.07 us -> 5.54 us
  waiting for transfers between devices: 9.17 us -> 9.95 us
    all_gather x1 -> x0, blocking collectives: 15.1 us -> none  [body(): gathered = lax.all_gather(queries, 'seq', axis=0, tiled=True)]
    all_to_all x0 -> x1, starting transfers between devices: none -> 6.35 us  [body(): gathered = jnp.concatenate(lax.all_to_all(outgoing, 'seq', 0, 0), axis=0)]
    slice x1, local copies, waits for them, and re-layouts: 8.1 us -> 4.46 us  [body(): shared_prefix_values[:, kv_head]]
    dot_general x4, matrix products: 5.26 us -> 8.35 us  [prefix_block(): lax.dot_general(query_rows, block_keys, (((1,), (1,)), ((), ())), preferr...]
    dot_general x4, matrix products: 1.43 us -> 4 us  [prefix_block(): outputs = jnp.dot(weights, block_values, preferred_element_type=jnp.float32)]
    reduce_sum x4, other arithmetic: 1.19 us -> 3.68 us  [prefix_block(): totals = jnp.sum(weights, axis=1, dtype=jnp.float32)]
    unnamed x24 -> x26, local copies, waits for them, and re-layouts: 4.02 us -> 1.55 us
    another operation x0 -> x1, local copies, waits for them, and re-layouts: none -> 1.5 us  [body(): outgoing = jnp.stack([queries] * lax.axis_size('seq'))]
  transfers between devices with their start and end apart: 3 -> 4, of which waited for: 2 -> 3; matrix products, arithmetic and copies ran while one was open for 20% -> 33% of each run, Pallas kernels for 0% -> 0%
where the time goes in v1:
time: 68.7 us; the launch traced here: 68.1 us
  starting transfers between devices  19.3 us (28%)
  local copies, waits for them, and re-layouts  18.9 us (28%)
  matrix products  14.1 us (21%)
  waiting for transfers between devices  9.95 us (14%)
  other arithmetic  5.54 us (8%)
    slice x1, local copies, waits for them, and re-layouts, body(): shared_prefix_keys[:, kv_head]  9.15 us
    dot_general x4, matrix products, prefix_block(): lax.dot_general(query_rows, block_keys, (((1,), (1,)), ((), ())), preferr...  8.35 us
    all_to_all x1, starting transfers between devices, body(): gathered = jnp.concatenate(lax.all_to_all(outgoing, 'seq', 0, 0), axis=0)  6.35 us
    all_to_all x1, waiting for transfers between devices, body(): lax.all_to_all(block_out.reshape(seq_count, own_count, head_count, width)...  5.93 us
    all_to_all x1, starting transfers between devices, body(): lax.all_to_all(block_total.reshape(state_shape), 'seq', split_axis=0, con...  5.08 us
    all_to_all x1, starting transfers between devices, body(): lax.all_to_all(block_max.reshape(state_shape), 'seq', split_axis=0, conca...  4.49 us
    slice x1, local copies, waits for them, and re-layouts, body(): shared_prefix_values[:, kv_head]  4.46 us
    dot_general x4, matrix products, prefix_block(): outputs = jnp.dot(weights, block_values, preferred_element_type=jnp.float32)  4 us
  transfers between devices with their start and end apart: 4, of which 3 were waited for; matrix products, arithmetic and copies ran while one was open for 33% of the time, Pallas kernels for 0%

profile of v1, /device:TPU:0, one launch (start us, length us, event | category | flops | bytes accessed | tf_op | source)
XLA Modules:
  0.0 68.1 jit_solution(2832082392285049380)
XLA Ops:
  0.0 1.5 %stack.16 = bf16[4,4,32,128]{3,2,1,0:T(8,128)(2,1)} broadcast(bf16[4,32,128]{2,1,0:T(8,128)(2,1)} %param.8), dimensions={1,2,3} | broadcast | bytes 163840 | tf_op jit(solution)/shard_map/stack | solution.py:37
  1.5 6.3 %all-to-all-start = ((bf16[4,4,32,128]{3,2,1,0:T(8,128)(2,1)}), bf16[4,4,32,128]{3,2,1,0:T(8,128)(2,1)S(1)}, u32[]{:S(2)}, u32[]{:S(2)}) async-start(bf16[4,4,32,128]{3,2,1,0:T(8,128)(2,1)} %stack.16), calls=%async_computation | async-start | bytes 262144 | tf_op jit(solution)/shard_map/all_to_all | solution.py:38
  7.9 9.1 %fusion.19 = (bf16[2048,1,128]{2,1,0:T(2,128)(2,1)}, bf16[2048,1,128]{2,1,0:T(2,128)(2,1)}, bf16[2048,1,128]{2,1,0:T(2,128)(2,1)}, bf16[2048,1,128]{2,1,0:T(2,128)(2,1)}) fusion(bf16[2048,4,128]{2,1,0:T(4,128)(2,1)} %param.11), kind=kLoop, calls=%fused_computation.62 | loop fusion | bytes 4194304 | tf_op jit(solution)/shard_map/slice | solution.py:47
  18.2 4.5 %fusion.20 = (bf16[2048,1,128]{2,1,0:T(2,128)(2,1)}, bf16[2048,1,128]{2,1,0:T(2,128)(2,1)}, bf16[2048,1,128]{2,1,0:T(2,128)(2,1)}, bf16[2048,1,128]{2,1,0:T(2,128)(2,1)}) fusion(bf16[2048,4,128]{2,1,0:T(4,128)(2,1)S(1)} %copy-done.3), kind=kLoop, calls=%fused_computation.63 | loop fusion | bytes 4194304 | tf_op jit(solution)/shard_map/slice | solution.py:47
  22.8 1.6 %fusion.24 = (f32[128]{0:T(128)S(1)}, f32[128,2048]{1,0:T(8,128)S(1)}) fusion(bf16[2048,1,128]{2,1,0:T(2,128)(2,1)} %get-tuple-element.11, bf16[16,4,8,128]{3,2,1,0:T(8,128)(2,1)S(1)} %bitcast.98), kind=kOutput, calls=%fused_computation.67 | convolution fusion | flops 67633024 | bytes 1606144 | tf_op jit(solution)/shard_map/dot_general | solution.py:10
  24.9 1.6 %fusion.23 = (f32[128]{0:T(128)S(1)}, f32[128,2048]{1,0:T(8,128)S(1)}) fusion(bf16[2048,1,128]{2,1,0:T(2,128)(2,1)} %get-tuple-element.13, bf16[16,4,8,128]{3,2,1,0:T(8,128)(2,1)S(1)} %bitcast.99), kind=kOutput, calls=%fused_computation.66 | convolution fusion | flops 67633024 | bytes 1606144 | tf_op jit(solution)/shard_map/dot_general | solution.py:10
  27.0 2.6 %fusion.22 = (f32[128]{0:T(128)S(1)}, f32[128,2048]{1,0:T(8,128)}) fusion(bf16[2048,1,128]{2,1,0:T(2,128)(2,1)} %get-tuple-element.12, bf16[16,4,8,128]{3,2,1,0:T(8,128)(2,1)S(1)} %bitcast.100), kind=kOutput, calls=%fused_computation.65 | convolution fusion | flops 67633024 | bytes 1606144 | tf_op jit(solution)/shard_map/dot_general | solution.py:10
  29.6 1.5 %convert_reduce_fusion.1 = f32[128]{0:T(128)S(1)} fusion(f32[128,2048]{1,0:T(8,128)} %get-tuple-element.22, f32[128]{0:T(128)S(1)} %get-tuple-element.21), kind=kLoop, calls=%fused_computation.16 | loop fusion | flops 1048448 | bytes 1049600 | tf_op jit(solution)/shard_map/reduce_sum | solution.py:17
  31.2 2.6 %fusion.21 = (f32[128]{0:T(128)S(1)}, f32[128,2048]{1,0:T(8,128)}) fusion(bf16[2048,1,128]{2,1,0:T(2,128)(2,1)} %get-tuple-element.14, bf16[16,4,8,128]{3,2,1,0:T(8,128)(2,1)S(1)} %bitcast.101), kind=kOutput, calls=%fused_computation.64 | convolution fusion | flops 67633024 | bytes 1606144 | tf_op jit(solution)/shard_map/dot_general | solution.py:10
  33.8 1.5 %convert_reduce_fusion = f32[128]{0:T(128)S(1)} fusion(f32[128,2048]{1,0:T(8,128)} %get-tuple-element.20, f32[128]{0:T(128)S(1)} %get-tuple-element.19), kind=kLoop, calls=%fused_computation.15 | loop fusion | flops 1048448 | bytes 1049600 | tf_op jit(solution)/shard_map/reduce_sum | solution.py:17
  35.6 0.7 reshape.114
  36.3 5.1 %all-to-all-start.3 = ((f32[4,1,128]{2,1,0:T(1,128)}), f32[4,1,128]{2,1,0:T(1,128)S(1)}, u32[]{:S(2)}, u32[]{:S(2)}) async-start(f32[4,1,128]{2,1,0:T(1,128)} %reshape.114), calls=%async_computation.3 | async-start | bytes 4096 | tf_op jit(solution)/shard_map/all_to_all | solution.py:106
  41.4 1.7 %convolution_bitcast_fusion.3 = f32[16,1,8,128]{3,2,0,1:T(8,128)S(1)} fusion(bf16[2048,1,128]{2,1,0:T(2,128)(2,1)} %get-tuple-element.15, f32[128,2048]{1,0:T(8,128)S(1)} %get-tuple-element.26, f32[128]{0:T(128)S(1)} %get-tuple-element.25), kind=kOutput, calls=%fused_computation.8 | convolution fusion | flops 67633152 | bytes 1638912 | tf_op jit(solution)/shard_map/dot_general | solution.py:18
  43.1 1.6 %convolution_bitcast_fusion.2 = f32[16,1,8,128]{3,2,0,1:T(8,128)S(1)} fusion(bf16[2048,1,128]{2,1,0:T(2,128)(2,1)} %get-tuple-element.17, f32[128,2048]{1,0:T(8,128)S(1)} %get-tuple-element.24, f32[128]{0:T(128)S(1)} %get-tuple-element.23), kind=kOutput, calls=%fused_computation.7 | convolution fusion | flops 67633152 | bytes 1638912 | tf_op jit(solution)/shard_map/dot_general | solution.py:18
  45.6 0.7 reshape.112
  46.2 0.6 all-to-all-done.3
  46.8 4.5 %all-to-all-start.1 = ((f32[4,1,128]{2,1,0:T(1,128)}), f32[4,1,128]{2,1,0:T(1,128)S(1)}, u32[]{:S(2)}, u32[]{:S(2)}) async-start(f32[4,1,128]{2,1,0:T(1,128)} %reshape.112), calls=%async_computation.1 | async-start | bytes 4096 | tf_op jit(solution)/shard_map/all_to_all | solution.py:103
  51.4 0.7 %copy.26 = f32[16,4,8,128]{3,2,1,0:T(8,128)} copy(f32[16,4,8,128]{3,2,0,1:T(8,128)S(1)} %pad_maximum_fusion) | data formatting | bytes 524288 | tf_op jit(solution)/shard_map/stack | solution.py:54
  52.6 0.7 reduce
  53.3 3.4 %all-to-all-done.1 = f32[4,1,128]{2,1,0:T(1,128)S(1)} async-done(((f32[4,1,128]{2,1,0:T(1,128)}), f32[4,1,128]{2,1,0:T(1,128)S(1)}, u32[]{:S(2)}, u32[]{:S(2)}) %all-to-all-start.1) | async-done | bytes 2080 | tf_op jit(solution)/shard_map/all_to_all | solution.py:103
  56.8 3.4 %all-to-all-start.2 = ((f32[4,4,32,128]{3,2,1,0:T(8,128)}), f32[4,4,32,128]{3,2,1,0:T(8,128)S(1)}, u32[]{:S(2)}, u32[]{:S(2)}) async-start(f32[4,4,32,128]{3,2,1,0:T(8,128)} %bitcast.30), calls=%async_computation.2 | async-start | bytes 524288 | tf_op jit(solution)/shard_map/all_to_all | solution.py:96
  60.2 0.7 reduce.1
  61.0 5.9 %all-to-all-done.2 = f32[4,4,32,128]{3,2,1,0:T(8,128)S(1)} async-done(((f32[4,4,32,128]{3,2,1,0:T(8,128)}), f32[4,4,32,128]{3,2,1,0:T(8,128)S(1)}, u32[]{:S(2)}, u32[]{:S(2)}) %all-to-all-start.2) | async-done | bytes 262176 | tf_op jit(solution)/shard_map/all_to_all | solution.py:96
  67.1 1.0 %fusion.4 = bf16[4,32,128]{2,1,0:T(8,128)(2,1)} fusion(f32[4,32,128]{2,1,0:T(8,128)S(1)} %multiply_reduce_fusion, bf16[4,192,4,128]{3,2,1,0:T(4,128)(2,1)S(1)} %copy-done.8, f32[4,32]{1,0:T(4,128)S(1)} %get-tuple-element.5, f32[4,32]{1,0:T(4,128)S(1)} %get-tuple-element.6, f32[4,4,128]{2,1,0:T(4,128)S(1)} %convert_element_type.46, ...), kind=kOutput, calls=%fused_computation.14 | convolution fusion | flops 6488064 | bytes 994048 | tf_op jit(solution)/shard_map/bgqs,bsgd->bgqd/dot_general | solution.py:80
  (60 shorter events, 4.4 us)
Async XLA Ops:
  0.0 17.3 %copy-start = (bf16[4,192,4,128]{3,2,1,0:T(4,128)(2,1)S(1)}, bf16[4,192,4,128]{3,2,1,0:T(4,128)(2,1)}, u32[]{:S(2)}) copy-start(bf16[4,192,4,128]{3,2,1,0:T(4,128)(2,1)} %param.13) | copy-start | bytes 2359300
  1.5 21.3 %all-to-all-start = ((bf16[4,4,32,128]{3,2,1,0:T(8,128)(2,1)}), bf16[4,4,32,128]{3,2,1,0:T(8,128)(2,1)S(1)}, u32[]{:S(2)}, u32[]{:S(2)}) async-start(bf16[4,4,32,128]{3,2,1,0:T(8,128)(2,1)} %stack.16), calls=%async_computation | async-start | bytes 262144 | tf_op jit(solution)/shard_map/all_to_all | solution.py:38
  7.9 9.2 %copy-start.6 = (bf16[4,32,128]{2,1,0:T(8,128)(2,1)S(1)}, bf16[4,32,128]{2,1,0:T(8,128)(2,1)}, u32[]{:S(2)}) copy-start(bf16[4,32,128]{2,1,0:T(8,128)(2,1)} %param.8) | copy-start | bytes 98308
  7.9 9.2 %copy-start.9 = (bf16[4,4,128]{2,1,0:T(4,128)(2,1)S(1)}, bf16[4,4,128]{2,1,0:T(4,128)(2,1)}, u32[]{:S(2)}) copy-start(bf16[4,4,128]{2,1,0:T(4,128)(2,1)} %param.9) | copy-start | bytes 12292
  7.9 9.3 %copy-start.10 = (s32[4]{0:T(128)S(1)}, s32[4]{0:T(128)}, u32[]{:S(2)}) copy-start(s32[4]{0:T(128)} %param.15) | copy-start | bytes 52
  7.9 10.3 %copy-start.3 = (bf16[2048,4,128]{2,1,0:T(4,128)(2,1)S(1)}, bf16[2048,4,128]{2,1,0:T(4,128)(2,1)}, u32[]{:S(2)}) copy-start(bf16[2048,4,128]{2,1,0:T(4,128)(2,1)} %param.12) | copy-start | bytes 6291460
  18.2 4.6 %copy-start.7 = (bf16[4,4,128]{2,1,0:T(4,128)(2,1)S(1)}, bf16[4,4,128]{2,1,0:T(4,128)(2,1)}, u32[]{:S(2)}) copy-start(bf16[4,4,128]{2,1,0:T(4,128)(2,1)} %param.10) | copy-start | bytes 12292
  36.3 10.6 %all-to-all-start.3 = ((f32[4,1,128]{2,1,0:T(1,128)}), f32[4,1,128]{2,1,0:T(1,128)S(1)}, u32[]{:S(2)}, u32[]{:S(2)}) async-start(f32[4,1,128]{2,1,0:T(1,128)} %reshape.114), calls=%async_computation.3 | async-start | bytes 4096 | tf_op jit(solution)/shard_map/all_to_all | solution.py:106
  41.3 3.3 %copy-start.1 = (f32[128,2048]{1,0:T(8,128)S(1)}, f32[128,2048]{1,0:T(8,128)}, u32[]{:S(2)}) copy-start(f32[128,2048]{1,0:T(8,128)} %get-tuple-element.22) | copy-start | bytes 3145732
  41.3 3.3 %copy-start.5 = (bf16[2048,1,128]{2,1,0:T(2,128)(2,1)S(1)}, bf16[2048,1,128]{2,1,0:T(2,128)(2,1)}, u32[]{:S(2)}) copy-start(bf16[2048,1,128]{2,1,0:T(2,128)(2,1)} %get-tuple-element.16) | copy-start | bytes 1572868
  41.3 3.7 %copy-start.2 = (f32[128,2048]{1,0:T(8,128)S(1)}, f32[128,2048]{1,0:T(8,128)}, u32[]{:S(2)}) copy-start(f32[128,2048]{1,0:T(8,128)} %get-tuple-element.20) | copy-start | bytes 3145732
  41.4 3.7 %copy-start.4 = (bf16[2048,1,128]{2,1,0:T(2,128)(2,1)S(1)}, bf16[2048,1,128]{2,1,0:T(2,128)(2,1)}, u32[]{:S(2)}) copy-start(bf16[2048,1,128]{2,1,0:T(2,128)(2,1)} %get-tuple-element.18) | copy-start | bytes 1572868
  45.1 22.0 %copy-start.8 = (bf16[4,192,4,128]{3,2,1,0:T(4,128)(2,1)S(1)}, bf16[4,192,4,128]{3,2,1,0:T(4,128)(2,1)}, u32[]{:S(2)}) copy-start(bf16[4,192,4,128]{3,2,1,0:T(4,128)(2,1)} %param.14) | copy-start | bytes 2359300
  46.8 9.9 %all-to-all-start.1 = ((f32[4,1,128]{2,1,0:T(1,128)}), f32[4,1,128]{2,1,0:T(1,128)S(1)}, u32[]{:S(2)}, u32[]{:S(2)}) async-start(f32[4,1,128]{2,1,0:T(1,128)} %reshape.112), calls=%async_computation.1 | async-start | bytes 4096 | tf_op jit(solution)/shard_map/all_to_all | solution.py:103
  56.8 10.2 %all-to-all-start.2 = ((f32[4,4,32,128]{3,2,1,0:T(8,128)}), f32[4,4,32,128]{3,2,1,0:T(8,128)S(1)}, u32[]{:S(2)}, u32[]{:S(2)}) async-start(f32[4,4,32,128]{3,2,1,0:T(8,128)} %bitcast.30), calls=%async_computation.2 | async-start | bytes 524288 | tf_op jit(solution)/shard_map/all_to_all | solution.py:96
